TPU v7x, 32 devices: a whole 2x2x4 slice. The times are simulated.
32 devices in a mesh: data: 8 (over z, y), width: 4 (over x, core).
Axes of the slice: x: 2, y: 2, z: 4, core: 2. Of those that a mesh axis runs over, the one named last changes fastest.
Arguments:
- grad_up: float32 [8, 768, 3072], P('data', None, 'width'), may hold values from -4 to 4
- grad_down: float32 [8, 3072, 768], P('data', 'width'), may hold values from -4 to 4
- grad_query: float32 [8, 768, 768], P('data', None, 'width'), may hold values from -4 to 4
- grad_key: float32 [8, 768, 768], P('data', None, 'width'), may hold values from -4 to 4
- grad_value: float32 [8, 768, 768], P('data', None, 'width'), may hold values from -4 to 4
- grad_mixed: float32 [8, 768, 768], P('data', 'width'), may hold values from -4 to 4
- grad_norm: float32 [8, 768], P('data'), may hold values from -8 to 8
- weight_up: float32 [768, 3072], P('data', 'width'), may hold values from -0.21875 to 0.21875
- weight_down: float32 [3072, 768], P('width', 'data'), may hold values from -0.109375 to 0.109375
- weight_query: float32 [768, 768], P('data', 'width'), may hold values from -0.21875 to 0.21875
- weight_key: float32 [768, 768], P('data', 'width'), may hold values from -0.21875 to 0.21875
- weight_value: float32 [768, 768], P('data', 'width'), may hold values from -0.21875 to 0.21875
- weight_mixed: float32 [768, 768], P('width', 'data'), may hold values from -0.21875 to 0.21875
- weight_norm: float32 [768], P('data'), may hold values from 0.25 to 1.75
- moment_up: float32 [768, 3072], P('data', 'width'), may hold values from 0.05 to 0.8
- moment_down: float32 [3072, 768], P('width', 'data'), may hold values from 0.05 to 0.8
- moment_query: float32 [768, 768], P('data', 'width'), may hold values from 0.05 to 0.8
- moment_key: float32 [768, 768], P('data', 'width'), may hold values from 0.05 to 0.8
- moment_value: float32 [768, 768], P('data', 'width'), may hold values from 0.05 to 0.8
- moment_mixed: float32 [768, 768], P('width', 'data'), may hold values from 0.05 to 0.8
- moment_norm: float32 [768], P('data'), may hold values from 0.05 to 0.8
Outputs:
- copy_up: bfloat16 [768, 3072], P(None, 'width')
- copy_down: bfloat16 [3072, 768], P('width')
- copy_query: bfloat16 [768, 768], P(None, 'width')
- copy_key: bfloat16 [768, 768], P(None, 'width')
- copy_value: bfloat16 [768, 768], P(None, 'width')
- copy_mixed: bfloat16 [768, 768], P('width')
- copy_norm: bfloat16 [768], replicated
- new_up: float32 [768, 3072], P('data', 'width')
- new_down: float32 [3072, 768], P('width', 'data')
- new_query: float32 [768, 768], P('data', 'width')
- new_key: float32 [768, 768], P('data', 'width')
- new_value: float32 [768, 768], P('data', 'width')
- new_mixed: float32 [768, 768], P('width', 'data')
- new_norm: float32 [768], P('data')
- state_new_up: float32 [768, 3072], P('data', 'width')
- state_new_down: float32 [3072, 768], P('width', 'data')
- state_new_query: float32 [768, 768], P('data', 'width')
- state_new_key: float32 [768, 768], P('data', 'width')
- state_new_value: float32 [768, 768], P('data', 'width')
- state_new_mixed: float32 [768, 768], P('width', 'data')
- state_new_norm: float32 [768], P('data')
All inputs are finite; a program needn't handle non-finite values.
Results may differ from a plain program's by a relative error of at most 0.0004.
Values may be sent and summed in bfloat16 or wider, within the bound.
A program may use at most 128 MiB of HBM per device.

v0:
```python
import jax
import jax.numpy as jnp
from jax import lax
from jax.sharding import PartitionSpec as P

learn_rate = 0.05
hold_rate = 0.9


def on_device(
    grad_up,
    grad_down,
    grad_query,
    grad_key,
    grad_value,
    grad_mixed,
    grad_norm,
    weight_up,
    weight_down,
    weight_query,
    weight_key,
    weight_value,
    weight_mixed,
    weight_norm,
    moment_up,
    moment_down,
    moment_query,
    moment_key,
    moment_value,
    moment_mixed,
    moment_norm,
):
    mean_up, mean_down, mean_query, mean_key, mean_value, mean_mixed, mean_norm = (
        lax.psum_scatter(grad_up[0], "data", scatter_dimension=0, tiled=True),
        lax.psum_scatter(grad_down[0], "data", scatter_dimension=1, tiled=True),
        lax.psum_scatter(grad_query[0], "data", scatter_dimension=0, tiled=True),
        lax.psum_scatter(grad_key[0], "data", scatter_dimension=0, tiled=True),
        lax.psum_scatter(grad_value[0], "data", scatter_dimension=0, tiled=True),
        lax.psum_scatter(grad_mixed[0], "data", scatter_dimension=1, tiled=True),
        lax.psum_scatter(grad_norm[0], "data", scatter_dimension=0, tiled=True),
    )
    mean_rate = lax.axis_size("data") ** (-0.5)
    mean_up = mean_up * mean_rate
    mean_down = mean_down * mean_rate
    mean_query = mean_query * mean_rate
    mean_key = mean_key * mean_rate
    mean_value = mean_value * mean_rate
    mean_mixed = mean_mixed * mean_rate
    mean_norm = mean_norm * mean_rate
    state_new_up = hold_rate * moment_up + (1.0 - hold_rate) * mean_up * mean_up
    new_up = weight_up - learn_rate * mean_up * lax.rsqrt(state_new_up + 1e-06)
    state_new_down = hold_rate * moment_down + (1.0 - hold_rate) * mean_down * mean_down
    new_down = weight_down - learn_rate * mean_down * lax.rsqrt(state_new_down + 1e-06)
    state_new_query = hold_rate * moment_query + (1.0 - hold_rate) * mean_query * mean_query
    new_query = weight_query - learn_rate * mean_query * lax.rsqrt(state_new_query + 1e-06)
    state_new_key = hold_rate * moment_key + (1.0 - hold_rate) * mean_key * mean_key
    new_key = weight_key - learn_rate * mean_key * lax.rsqrt(state_new_key + 1e-06)
    state_new_value = hold_rate * moment_value + (1.0 - hold_rate) * mean_value * mean_value
    new_value = weight_value - learn_rate * mean_value * lax.rsqrt(state_new_value + 1e-06)
    state_new_mixed = hold_rate * moment_mixed + (1.0 - hold_rate) * mean_mixed * mean_mixed
    new_mixed = weight_mixed - learn_rate * mean_mixed * lax.rsqrt(state_new_mixed + 1e-06)
    state_new_norm = hold_rate * moment_norm + (1.0 - hold_rate) * mean_norm * mean_norm
    new_norm = weight_norm - learn_rate * mean_norm * lax.rsqrt(state_new_norm + 1e-06)
    copy_up, copy_down, copy_query, copy_key, copy_value, copy_mixed, copy_norm = (
        lax.all_gather(new_up.astype(jnp.bfloat16), "data", axis=0, tiled=True),
        lax.all_gather(new_down.astype(jnp.bfloat16), "data", axis=1, tiled=True),
        lax.all_gather(new_query.astype(jnp.bfloat16), "data", axis=0, tiled=True),
        lax.all_gather(new_key.astype(jnp.bfloat16), "data", axis=0, tiled=True),
        lax.all_gather(new_value.astype(jnp.bfloat16), "data", axis=0, tiled=True),
        lax.all_gather(new_mixed.astype(jnp.bfloat16), "data", axis=1, tiled=True),
        lax.all_gather(new_norm.astype(jnp.bfloat16), "data", axis=0, tiled=True),
    )
    return (
        copy_up,
        copy_down,
        copy_query,
        copy_key,
        copy_value,
        copy_mixed,
        copy_norm,
        new_up,
        new_down,
        new_query,
        new_key,
        new_value,
        new_mixed,
        new_norm,
        state_new_up,
        state_new_down,
        state_new_query,
        state_new_key,
        state_new_value,
        state_new_mixed,
        state_new_norm,
    )


def solution(mesh):
    return jax.shard_map(
        on_device,
        mesh=mesh,
        in_specs=(
            P("data", None, "width"),
            P("data", "width", None),
            P("data", None, "width"),
            P("data", None, "width"),
            P("data", None, "width"),
            P("data", "width", None),
            P("data", None),
            P("data", "width"),
            P("width", "data"),
            P("data", "width"),
            P("data", "width"),
            P("data", "width"),
            P("width", "data"),
            P("data"),
            P("data", "width"),
            P("width", "data"),
            P("data", "width"),
            P("data", "width"),
            P("data", "width"),
            P("width", "data"),
            P("data"),
        ),
        out_specs=(
            P(None, "width"),
            P("width", None),
            P(None, "width"),
            P(None, "width"),
            P(None, "width"),
            P("width", None),
            P(),
            P("data", "width"),
            P("width", "data"),
            P("data", "width"),
            P("data", "width"),
            P("data", "width"),
            P("width", "data"),
            P("data"),
            P("data", "width"),
            P("width", "data"),
            P("data", "width"),
            P("data", "width"),
            P("data", "width"),
            P("width", "data"),
            P("data"),
        ),
        check_vma=False,
    )
```

profile of v0, /device:TPU:0, one launch (start us, length us, event | category | flops | bytes accessed | tf_op | source)
XLA Modules:
  0.0 516.1 jit_solution(12542500748333698461)
XLA Ops:
  8.0 0.9 copy-done
  8.9 2.0 copy.50
  11.0 1.0 copy-done.2
  11.9 1.1 copy.51
  13.2 1.1 copy.52
  14.4 1.2 copy.53
  15.7 1.2 copy.60
  16.9 67.3 %reduce-scatter.9.cloned.1.call-done = f32[96,768]{1,0:T(8,128)} async-done(((f32[768,768]{1,0:T(8,128)}), f32[96,768]{1,0:T(8,128)}) %reduce-scatter.9.cloned.1.call-update) | async-done | bytes 294928 | tf_op jit(solution)/shard_map/reduce_scatter | solution.py:34
  84.3 1.9 fusion.6
  86.3 70.3 %reduce-scatter.11.cloned.1.call-done = f32[768,96]{0,1:T(8,128)} async-done(((f32[768,768]{0,1:T(8,128)}), f32[768,96]{0,1:T(8,128)}) %reduce-scatter.11.cloned.1.call-update) | async-done | bytes 294928 | tf_op jit(solution)/shard_map/reduce_scatter | solution.py:35
  156.6 1.9 fusion.5
  160.5 19.3 %all-reduce.1 = f32[768]{0:T(1024)S(1)} all-reduce(f32[768]{0:T(1024)S(1)} %reduce), channel_id=8, replica_groups=mesh['data'=8,'width'=4] {'data'}, use_global_device_ids=true, to_apply=%region_6.0.clone | all-reduce | flops 768 | bytes 6144
  180.7 17.7 %all-reduce = bf16[768]{0:T(1024)(128)(2,1)} all-reduce(bf16[768]{0:T(1024)(128)(2,1)S(1)} %dynamic-update-slice), channel_id=1, replica_groups=mesh['data'=8,'width'=4] {'data'}, use_global_device_ids=true, to_apply=%add | all-reduce | flops 768 | bytes 3072
  198.4 24.7 %reduce-scatter.13.cloned.1.call-done = f32[96,192]{1,0:T(8,128)} async-done(((f32[768,192]{1,0:T(8,128)}), f32[96,192]{1,0:T(8,128)}) %reduce-scatter.13.cloned.1.call-update) | async-done | bytes 73744 | tf_op jit(solution)/shard_map/reduce_scatter | solution.py:36
  223.1 1.6 fusion.4
  224.7 31.5 %all_gather.23 = bf16[768,192]{1,0:T(8,128)(2,1)S(1)} all-gather(bf16[96,192]{1,0:T(8,128)(2,1)S(1)} %get-tuple-element.75), channel_id=1, replica_groups=mesh['data'=8,'width'=4] {'data'}, dimensions={0}, use_global_device_ids=true | all-gather | bytes 331776 | tf_op jit(solution)/shard_map/all_gather | solution.py:67
  256.2 0.9 copy.56
  257.0 32.2 %reduce-scatter.15.cloned.1.call-done = f32[96,192]{1,0:T(8,128)} async-done(((f32[768,192]{1,0:T(8,128)}), f32[96,192]{1,0:T(8,128)}) %reduce-scatter.15.cloned.1.call-update) | async-done | bytes 73744 | tf_op jit(solution)/shard_map/reduce_scatter | solution.py:37
  289.2 1.6 fusion.3
  290.8 31.8 %all_gather.24 = bf16[768,192]{1,0:T(8,128)(2,1)S(1)} all-gather(bf16[96,192]{1,0:T(8,128)(2,1)S(1)} %get-tuple-element.72), channel_id=1, replica_groups=mesh['data'=8,'width'=4] {'data'}, dimensions={0}, use_global_device_ids=true | all-gather | bytes 331776 | tf_op jit(solution)/shard_map/all_gather | solution.py:68
  322.6 0.9 copy.57
  323.5 31.5 %reduce-scatter.17.cloned.1.call-done = f32[96,192]{1,0:T(8,128)} async-done(((f32[768,192]{1,0:T(8,128)}), f32[96,192]{1,0:T(8,128)}) %reduce-scatter.17.cloned.1.call-update) | async-done | bytes 73744 | tf_op jit(solution)/shard_map/reduce_scatter | solution.py:38
  355.0 1.6 fusion.2
  356.6 31.6 %all_gather.25 = bf16[768,192]{1,0:T(8,128)(2,1)S(1)} all-gather(bf16[96,192]{1,0:T(8,128)(2,1)S(1)} %get-tuple-element.69), channel_id=1, replica_groups=mesh['data'=8,'width'=4] {'data'}, dimensions={0}, use_global_device_ids=true | all-gather | bytes 331776 | tf_op jit(solution)/shard_map/all_gather | solution.py:69
  388.2 0.9 copy.58
  389.1 31.7 %reduce-scatter.19.cloned.1.call-done = f32[96,192]{1,0:T(8,128)} async-done(((f32[768,192]{1,0:T(8,128)}), f32[96,192]{1,0:T(8,128)}) %reduce-scatter.19.cloned.1.call-update) | async-done | bytes 73744
  420.8 1.0 copy.61
  422.6 31.5 %all_gather.26 = bf16[192,768]{0,1:T(8,128)(2,1)S(1)} all-gather(bf16[192,96]{0,1:T(8,128)(2,1)S(1)} %copy.54), channel_id=1, replica_groups=mesh['data'=8,'width'=4] {'data'}, dimensions={1}, use_global_device_ids=true | all-gather | bytes 331776 | tf_op jit(solution)/shard_map/all_gather | solution.py:70
  455.0 8.8 %all-gather.3.cloned.1.call-done = bf16[768,768]{1,0:T(8,128)(2,1)} async-done(((bf16[96,768]{1,0:T(8,128)(2,1)}), bf16[768,768]{1,0:T(8,128)(2,1)}) %all-gather.3.cloned.1.call-update) | async-done | bytes 1179664 | tf_op jit(solution)/shard_map/all_gather | solution.py:65
  463.8 42.1 %all-gather.5.cloned.1.call-done = bf16[768,768]{0,1:T(8,128)(2,1)} async-done(((bf16[768,96]{0,1:T(8,128)(2,1)}), bf16[768,768]{0,1:T(8,128)(2,1)}) %all-gather.5.cloned.1.call-update) | async-done | bytes 1179664 | tf_op jit(solution)/shard_map/all_gather | solution.py:66
  505.9 2.4 copy.55
  508.3 1.0 copy.64
  (66 shorter events, 4.3 us)
Async XLA Ops:
  7.2 77.1 %reduce-scatter.9.cloned.1.call-start = ((), (), s32[]{:S(2)}) async-start(), calls=%async_computation.6 | async-start | bytes 2654208 | tf_op jit(solution)/shard_map/reduce_scatter | solution.py:34
  7.2 1.7 copy-start
  7.9 148.7 %reduce-scatter.11.cloned.1.call-start = ((), (), s32[]{:S(2)}) async-start(), calls=%async_computation.8 | async-start | bytes 2654208 | tf_op jit(solution)/shard_map/reduce_scatter | solution.py:35
  10.9 1.1 copy-start.2
  10.9 2.3 copy-start.3
  10.9 212.1 %reduce-scatter.13.cloned.1.call-start = ((), (), s32[]{:S(2)}) async-start(), calls=%async_computation.10 | async-start | bytes 884736 | tf_op jit(solution)/shard_map/reduce_scatter | solution.py:36
  13.1 1.3 copy-start.4
  13.1 276.1 %reduce-scatter.15.cloned.1.call-start = ((), (), s32[]{:S(2)}) async-start(), calls=%async_computation.11 | async-start | bytes 884736 | tf_op jit(solution)/shard_map/reduce_scatter | solution.py:37
  14.4 1.3 copy-start.5
  14.4 340.7 %reduce-scatter.17.cloned.1.call-start = ((), (), s32[]{:S(2)}) async-start(), calls=%async_computation.12 | async-start | bytes 884736 | tf_op jit(solution)/shard_map/reduce_scatter | solution.py:38
  15.6 68.7 %copy-start.6 = (f32[96,768]{1,0:T(8,128)S(1)}, f32[96,768]{1,0:T(8,128)}, u32[]{:S(2)}) copy-start(f32[96,768]{1,0:T(8,128)} %param.28) | copy-start | bytes 884740
  15.6 68.6 %copy-start.7 = (f32[96,768]{1,0:T(8,128)S(1)}, f32[96,768]{1,0:T(8,128)}, u32[]{:S(2)}) copy-start(f32[96,768]{1,0:T(8,128)} %param.35) | copy-start | bytes 884740
  15.6 405.2 %reduce-scatter.19.cloned.1.call-start = ((), (), s32[]{:S(2)}) async-start(), calls=%async_computation.13 | async-start | bytes 884736
  16.9 139.8 %copy-start.8 = (f32[768,96]{0,1:T(8,128)S(1)}, f32[768,96]{0,1:T(8,128)}, u32[]{:S(2)}) copy-start(f32[768,96]{0,1:T(8,128)} %param.29) | copy-start | bytes 884740
  16.9 139.8 %copy-start.9 = (f32[768,96]{0,1:T(8,128)S(1)}, f32[768,96]{0,1:T(8,128)}, u32[]{:S(2)}) copy-start(f32[768,96]{0,1:T(8,128)} %param.36) | copy-start | bytes 884740
  16.9 446.9 %all-gather.3.cloned.1.call-start = ((), (), s32[]{:S(2)}) async-start(), calls=%async_computation.7 | async-start | bytes 1327104 | tf_op jit(solution)/shard_map/all_gather | solution.py:65
  86.2 72.4 %copy-start.18 = (f32[1,768]{1,0:T(1,128)S(1)}, f32[1,768]{1,0:T(1,128)}, u32[]{:S(2)}) copy-start(f32[1,768]{1,0:T(1,128)} %param.27) | copy-start | bytes 9220
  86.2 72.4 %copy-start.19 = (u32[32]{0:T(128)S(1)}, u32[32]{0:T(128)}, u32[]{:S(2)}) copy-start(u32[32]{0:T(128)} %constant.53) | copy-start | bytes 388
  86.2 93.6 %copy-start.20 = (f32[96]{0:T(128)S(1)}, f32[96]{0:T(128)}, u32[]{:S(2)}) copy-start(f32[96]{0:T(128)} %param.34) | copy-start | bytes 1156
  86.2 93.6 %copy-start.21 = (f32[96]{0:T(128)S(1)}, f32[96]{0:T(128)}, u32[]{:S(2)}) copy-start(f32[96]{0:T(128)} %param.41) | copy-start | bytes 1156
  86.2 136.8 %copy-start.10 = (f32[96,192]{1,0:T(8,128)S(1)}, f32[96,192]{1,0:T(8,128)}, u32[]{:S(2)}) copy-start(f32[96,192]{1,0:T(8,128)} %param.30) | copy-start | bytes 221188
  86.2 136.8 %copy-start.11 = (f32[96,192]{1,0:T(8,128)S(1)}, f32[96,192]{1,0:T(8,128)}, u32[]{:S(2)}) copy-start(f32[96,192]{1,0:T(8,128)} %param.37) | copy-start | bytes 221188
  86.3 419.6 %all-gather.5.cloned.1.call-start = ((), (), s32[]{:S(2)}) async-start(), calls=%async_computation.9 | async-start | bytes 1327104 | tf_op jit(solution)/shard_map/all_gather | solution.py:66
  158.6 130.6 %copy-start.12 = (f32[96,192]{1,0:T(8,128)S(1)}, f32[96,192]{1,0:T(8,128)}, u32[]{:S(2)}) copy-start(f32[96,192]{1,0:T(8,128)} %param.31) | copy-start | bytes 221188
  158.6 130.6 %copy-start.13 = (f32[96,192]{1,0:T(8,128)S(1)}, f32[96,192]{1,0:T(8,128)}, u32[]{:S(2)}) copy-start(f32[96,192]{1,0:T(8,128)} %param.38) | copy-start | bytes 221188
  256.2 98.9 %copy-start.14 = (f32[96,192]{1,0:T(8,128)S(1)}, f32[96,192]{1,0:T(8,128)}, u32[]{:S(2)}) copy-start(f32[96,192]{1,0:T(8,128)} %param.32) | copy-start | bytes 221188
  256.2 98.9 %copy-start.15 = (f32[96,192]{1,0:T(8,128)S(1)}, f32[96,192]{1,0:T(8,128)}, u32[]{:S(2)}) copy-start(f32[96,192]{1,0:T(8,128)} %param.39) | copy-start | bytes 221188
  322.6 99.2 %copy-start.16 = (f32[192,96]{1,0:T(8,128)S(1)}, f32[192,96]{1,0:T(8,128)}, u32[]{:S(2)}) copy-start(f32[192,96]{1,0:T(8,128)} %param.33) | copy-start | bytes 221188
  322.6 99.2 %copy-start.17 = (f32[192,96]{1,0:T(8,128)S(1)}, f32[192,96]{1,0:T(8,128)}, u32[]{:S(2)}) copy-start(f32[192,96]{1,0:T(8,128)} %param.40) | copy-start | bytes 221188
  463.8 44.4 %copy-start.1 = (bf16[768,768]{1,0:T(8,128)(2,1)S(1)}, bf16[768,768]{1,0:T(8,128)(2,1)}, u32[]{:S(2)}) copy-start(bf16[768,768]{1,0:T(8,128)(2,1)} %all-gather.3.cloned.1.call-done) | copy-start | bytes 3538948
Sparse Core Ops, SparseCore 0:
  11.5 72.7 reduce-scatter.8
  87.8 68.8 reduce-scatter.10
  160.5 62.5 reduce-scatter.12
  226.8 62.3 reduce-scatter.14
  292.3 62.6 reduce-scatter.16
  358.2 62.5 reduce-scatter.18
  423.0 40.7 all-gather.2
  466.0 39.8 all-gather.4
where the time goes:
time: 517 us; the launch traced here: 516 us
  waiting for transfers between devices  309 us (60%)
  blocking collectives  163 us (32%)
  local copies, waits for them, and re-layouts  17.3 us (3%)
  between operations  15.7 us (3%)
  other arithmetic  9.98 us (2%)
    reduce_scatter x1, waiting for transfers between devices, on_device(): lax.psum_scatter(grad_down[0], 'data', scatter_dimension=1, tiled=True)  70.3 us
    reduce_scatter x1, waiting for transfers between devices, on_device(): lax.psum_scatter(grad_up[0], 'data', scatter_dimension=0, tiled=True)  67.3 us
    all_gather x1, waiting for transfers between devices, on_device(): lax.all_gather(new_down.astype(jnp.bfloat16), 'data', axis=1, tiled=True)  42.1 us
    unnamed x2, blocking collectives  37.1 us
    unnamed x9, waiting for transfers between devices  32.5 us
    reduce_scatter x1, waiting for transfers between devices, on_device(): lax.psum_scatter(grad_key[0], 'data', scatter_dimension=0, tiled=True)  32.2 us
    all_gather x1, blocking collectives, on_device(): lax.all_gather(new_key.astype(jnp.bfloat16), 'data', axis=0, tiled=True)  31.8 us
    all_gather x1, blocking collectives, on_device(): lax.all_gather(new_value.astype(jnp.bfloat16), 'data', axis=0, tiled=True)  31.6 us
  transfers between devices with their start and end apart: 8, of which 8 were waited for; matrix products, arithmetic and copies ran while one was open for 4% of the time, Pallas kernels for 0%

commit v1 on v0

v1 whole, which is shorter than its diff:
```python
import functools

import jax
import jax.numpy as jnp
from jax import lax
from jax.experimental import pallas as pl
from jax.experimental.pallas import tpu as pltpu
from jax.sharding import PartitionSpec as P

learn_rate = 0.05
hold_rate = 0.9
LANES = 128
SUB = 8


def round_up(value, unit):
    return -(-value // unit) * unit


def turn(block):
    rows, cols = block.shape
    tall, wide = round_up(rows, LANES), round_up(cols, LANES)
    if wide != cols:
        block = jnp.concatenate([block, jnp.zeros((rows, wide - cols), block.dtype)], axis=1)
    if tall != rows:
        block = jnp.concatenate([block, jnp.zeros((tall - rows, wide), block.dtype)], axis=0)
    return block.T[:cols, :rows]


def kernel(n, bits, rows, orders, *refs):
    refs = list(refs)
    take = lambda count: [refs.pop(0) for _ in range(count)]
    g_up, g_down, g_query, g_key, g_value, g_mixed, g_norm = take(7)
    w_up, w_down, w_query, w_key, w_value, w_mixed, w_norm = take(7)
    m_up, m_down, m_query, m_key, m_value, m_mixed, m_norm = take(7)
    c_up, c_down, c_query, c_key, c_value, c_mixed, c_norm = take(7)
    n_up, n_down, n_query, n_key, n_value, n_mixed, n_norm = take(7)
    s_up, s_down, s_query, s_key, s_value, s_mixed, s_norm = take(7)
    count = len(orders)
    part = take(count)
    held = [take(bits) for _ in range(count)]
    copies = take(count)
    send_sem, recv_sem = take(2)

    me = lax.axis_index("data")
    bit = [(me // 2**k) % 2 for k in range(bits)]
    partner = [me + 2**k * (1 - 2 * bit[k]) for k in range(bits)]

    barrier = pltpu.get_barrier_semaphore()
    for k in range(bits):
        pl.semaphore_signal(
            barrier, inc=1, device_id={"data": partner[k]}, device_id_type=pl.DeviceIdType.MESH
        )
    pl.semaphore_wait(barrier, bits)

    mean_rate = n ** (-0.5)
    half = g_up.shape[1] // 2
    heads = g_query.shape[1]
    mine = tuple(bit[k] for k in reversed(range(bits)))
    every = (slice(None),) * bits

    def index(chunk, step, own):
        fixed = {k: bit[k] for k in orders[chunk][:step]}
        if step < bits:
            k = orders[chunk][step]
            fixed[k] = bit[k] if own else 1 - bit[k]
        return tuple(fixed.get(k, slice(None)) for k in reversed(range(bits)))

    def copy(src, dst, chunk, slot, k):
        return pltpu.make_async_remote_copy(
            src_ref=src,
            dst_ref=dst,
            send_sem=send_sem.at[chunk, slot],
            recv_sem=recv_sem.at[chunk, slot],
            device_id={"data": partner[k]},
            device_id_type=pl.DeviceIdType.MESH,
        )

    def scatter(chunk, step):
        return copy(
            part[chunk].at[index(chunk, step, False)],
            held[chunk][step],
            chunk,
            step,
            orders[chunk][step],
        )

    def gather(chunk, step):
        there = copies[chunk].at[index(chunk, step, True)]
        return copy(there, there, chunk, bits + step, orders[chunk][step])

    def tile_loop(body):
        def step(i, carry):
            body(pl.multiple_of(i * SUB, SUB))
            return carry

        lax.fori_loop(0, rows // SUB, step, 0)

    def blocks(value):
        return value.reshape((2,) * bits + (rows, value.shape[-1]))

    def fill_up(h):
        def fill(chunk):
            for d in range(n):
                where = tuple((d >> k) & 1 for k in reversed(range(bits)))

                def body(r):
                    part[chunk][where + (pl.ds(r, SUB), slice(None))] = g_up[
                        pl.ds(pl.multiple_of(d * rows + r, SUB), SUB), h * half : (h + 1) * half
                    ]

                tile_loop(body)

        return fill

    def fill_down(h):
        def fill(chunk):
            for j in range(half // LANES):
                block = g_down[h * half + j * LANES : h * half + (j + 1) * LANES, :]
                part[chunk][every + (slice(None), slice(j * LANES, (j + 1) * LANES))] = blocks(turn(block))

        return fill

    def fill_pair(first, second, turned):
        def fill(chunk):
            for d in range(n):
                where = tuple((d >> k) & 1 for k in reversed(range(bits)))
                if turned is None:

                    def body(r):
                        at = pl.ds(pl.multiple_of(d * rows + r, SUB), SUB)
                        part[chunk][where + (pl.ds(r, SUB), slice(None))] = jnp.concatenate(
                            [first[at, :], second[at, :]], axis=1
                        )

                    tile_loop(body)
                else:
                    at = slice(d * rows, (d + 1) * rows)
                    part[chunk][where] = jnp.concatenate([first[at, :], turned[at, :]], axis=1)

        return fill

    def fill_norm(chunk):
        for d in range(n):
            where = tuple((d >> k) & 1 for k in reversed(range(bits)))
            part[chunk][where] = jnp.zeros_like(part[chunk][where])
            part[chunk][where + (slice(0, 1), slice(0, rows))] = g_norm[d : d + 1, :]

    def update(total, weight, moment):
        mean = total * mean_rate
        state = hold_rate * moment + (1.0 - hold_rate) * mean * mean
        return weight - learn_rate * mean * lax.rsqrt(state + 1e-06), state

    def own(chunk, lanes):
        return part[chunk][mine + (slice(None), lanes)]

    def step_up(h):
        def run(chunk):
            at = slice(h * half, (h + 1) * half)
            new, state = update(own(chunk, slice(None)), w_up[:, at], m_up[:, at])
            n_up[:, at] = new
            s_up[:, at] = state
            copies[chunk][mine] = new.astype(jnp.bfloat16)

        return run

    def step_down(h):
        def run(chunk):
            for j in range(half // LANES):
                lanes = slice(j * LANES, (j + 1) * LANES)
                at = slice(h * half + j * LANES, h * half + (j + 1) * LANES)
                new, state = update(own(chunk, lanes), turn(w_down[at, :]), turn(m_down[at, :]))
                copies[chunk][mine + (slice(None), lanes)] = new.astype(jnp.bfloat16)
                n_down[at, :] = turn(new)
                s_down[at, :] = turn(state)

        return run

    def step_query_key(chunk):
        weight = jnp.concatenate([w_query[...], w_key[...]], axis=1)
        moment = jnp.concatenate([m_query[...], m_key[...]], axis=1)
        new, state = update(own(chunk, slice(None)), weight, moment)
        copies[chunk][mine] = new.astype(jnp.bfloat16)
        n_query[...], n_key[...] = new[:, :heads], new[:, heads:]
        s_query[...], s_key[...] = state[:, :heads], state[:, heads:]

    def step_value_mixed(chunk):
        weight = jnp.concatenate([w_value[...], turn(w_mixed[...])], axis=1)
        moment = jnp.concatenate([m_value[...], turn(m_mixed[...])], axis=1)
        new, state = update(own(chunk, slice(None)), weight, moment)
        copies[chunk][mine] = new.astype(jnp.bfloat16)
        n_value[...], s_value[...] = new[:, :heads], state[:, :heads]
        n_mixed[...] = turn(new[:, heads:])
        s_mixed[...] = turn(state[:, heads:])

    def step_norm(chunk):
        new, state = update(part[chunk][mine][0:1, :rows], w_norm[...], m_norm[...])
        n_norm[...] = new
        s_norm[...] = state
        width = part[chunk].shape[-1]
        full = jnp.zeros((16, width), jnp.float32)
        if width != rows:
            new = jnp.concatenate([new, jnp.zeros((1, width - rows), jnp.float32)], axis=1)
        copies[chunk][mine] = (full + new).astype(jnp.bfloat16)

    group = 1 if rows % 16 == 0 else 2

    def end_rows(chunk, write):
        for d in range(0, n, group):
            got = [
                copies[chunk][tuple(((d + i) >> k) & 1 for k in reversed(range(bits)))] for i in range(group)
            ]
            if group > 1:
                got = [jnp.concatenate([g.astype(jnp.float32) for g in got], axis=0).astype(jnp.bfloat16)]
            write(slice(d * rows, (d + group) * rows), got[0])

    def end_up(h):
        def end(chunk):
            def write(at, value):
                c_up[at, h * half : (h + 1) * half] = value

            end_rows(chunk, write)

        return end

    def end_down(h):
        def end(chunk):
            for j in range(half // LANES):
                lanes = slice(j * LANES, (j + 1) * LANES)
                value = copies[chunk][every + (slice(None), lanes)].astype(jnp.float32)
                value = value.reshape(n * rows, LANES)
                c_down[h * half + j * LANES : h * half + (j + 1) * LANES, :] = turn(value).astype(jnp.bfloat16)

        return end

    def end_query_key(chunk):
        def write(at, value):
            value = value.astype(jnp.float32)
            c_query[at, :] = value[:, :heads].astype(jnp.bfloat16)
            c_key[at, :] = value[:, heads:].astype(jnp.bfloat16)

        end_rows(chunk, write)

    def end_value_mixed(chunk):
        def write(at, value):
            c_value[at, :] = value.astype(jnp.float32)[:, :heads].astype(jnp.bfloat16)

        end_rows(chunk, write)
        value = copies[chunk][...].astype(jnp.float32).reshape(n * rows, 2 * heads)
        c_mixed[...] = turn(value[:, heads:]).astype(jnp.bfloat16)

    def end_norm(chunk):
        got = [
            copies[chunk][tuple((d >> k) & 1 for k in reversed(range(bits)))].astype(jnp.float32)[0:1, :rows]
            for d in range(n)
        ]
        for d in range(n):
            c_norm[d : d + 1, :] = got[d]

    def fill_value_mixed(chunk):
        fill_pair(g_value, None, turn(g_mixed[...]))(chunk)

    plan = [
        (fill_up(0), step_up(0), end_up(0)),
        (fill_up(1), step_up(1), end_up(1)),
        (fill_norm, step_norm, end_norm),
        (fill_down(0), step_down(0), end_down(0)),
        (fill_down(1), step_down(1), end_down(1)),
        (fill_value_mixed, step_value_mixed, end_value_mixed),
        (fill_pair(g_query, g_key, None), step_query_key, end_query_key),
    ]

    for chunk in range(count):
        plan[chunk][0](chunk)
        scatter(chunk, 0).start()

    def event(chunk, stage):
        if stage < bits:
            scatter(chunk, stage).wait()
            where = index(chunk, stage, True)

            def body(r):
                at = pl.ds(r, SUB)
                full = where + (at, slice(None))
                lead = (slice(None),) * (len(held[chunk][stage].shape) - 2)
                part[chunk][full] = part[chunk][full] + held[chunk][stage][lead + (at, slice(None))]

            def step(i, carry):
                body(pl.multiple_of(i * SUB, SUB))
                return carry

            lax.fori_loop(0, part[chunk].shape[-2] // SUB, step, 0)
            if stage + 1 < bits:
                scatter(chunk, stage + 1).start()
            else:
                plan[chunk][1](chunk)
                gather(chunk, bits - 1).start()
        else:
            step = 2 * bits - 1 - stage
            gather(chunk, step).wait()
            if step > 0:
                gather(chunk, step - 1).start()
            else:
                plan[chunk][2](chunk)

    ahead = []
    for chunk in range(count):
        for stage in range(2 * bits):
            late = 0.5 * stage if stage < 2 * bits - 1 else max(0.5 * stage, count + 0.5 - 0.5 * chunk)
            ahead.append((chunk + late, chunk, stage))
    for _, chunk, stage in sorted(ahead):
        event(chunk, stage)


def solution(mesh):
    n = mesh.shape["data"]
    bits = n.bit_length() - 1

    def on_device(*args):
        grads, weights, moments = args[:7], args[7:14], args[14:]
        rows = weights[0].shape[0]
        grads = [g[0] for g in grads[:6]] + [grads[6].reshape(n, rows)]
        weights = list(weights[:6]) + [weights[6].reshape(1, rows)]
        moments = list(moments[:6]) + [moments[6].reshape(1, rows)]
        half, heads = grads[0].shape[1] // 2, grads[2].shape[1]
        near = tuple(range(bits))
        far = near[1:] + near[:1]
        wide = round_up(rows, LANES)
        sizes = [(rows, half)] * 2 + [(SUB, wide)] + [(rows, half)] * 2 + [(rows, 2 * heads)] * 2
        orders = [far] + [near] * 6
        copy_sizes = [s if i != 2 else (16, wide) for i, s in enumerate(sizes)]
        shape = lambda a, dtype: jax.ShapeDtypeStruct(a.shape, dtype)
        out_shape = (
            [shape(g, jnp.bfloat16) for g in grads[:6]]
            + [shape(grads[6], jnp.float32)]
            + [shape(w, jnp.float32) for w in weights]
            + [shape(w, jnp.float32) for w in weights]
        )
        scratch = [pltpu.VMEM((2,) * bits + s, jnp.float32) for s in sizes]
        for order, s in zip(orders, sizes):
            for step in range(bits):
                scratch.append(pltpu.VMEM((2,) * (bits - step - 1) + s, jnp.float32))
        scratch += [pltpu.VMEM((2,) * bits + s, jnp.bfloat16) for s in copy_sizes]
        scratch += [pltpu.SemaphoreType.DMA((len(sizes), 2 * bits))] * 2
        vmem = pl.BlockSpec(memory_space=pltpu.VMEM)
        outs = pl.pallas_call(
            functools.partial(kernel, n, bits, rows, orders),
            out_shape=out_shape,
            in_specs=[vmem] * 21,
            out_specs=[vmem] * 21,
            scratch_shapes=scratch,
            compiler_params=pltpu.CompilerParams(
                collective_id=0, has_side_effects=True, vmem_limit_bytes=60 * 2**20
            ),
        )(*grads, *weights, *moments)
        outs = list(outs)
        outs[6] = outs[6].reshape(-1).astype(jnp.bfloat16)
        outs[13] = outs[13].reshape(-1)
        outs[20] = outs[20].reshape(-1)
        return tuple(outs)

    row, col, vec = P("data", "width"), P("width", "data"), P("data")
    part = (row, col, row, row, row, col, vec)
    return jax.shard_map(
        on_device,
        mesh=mesh,
        in_specs=(
            P("data", None, "width"),
            P("data", "width", None),
            P("data", None, "width"),
            P("data", None, "width"),
            P("data", None, "width"),
            P("data", "width", None),
            P("data", None),
        )
        + part
        + part,
        out_specs=(
            P(None, "width"),
            P("width", None),
            P(None, "width"),
            P(None, "width"),
            P(None, "width"),
            P("width", None),
            P(),
        )
        + part
        + part,
        check_vma=False,
    )
```

time: 517 us -> 212 us (0.41)
  waiting for transfers between devices: 309 us -> 0 us
  Pallas kernels: 0 us -> 183 us
  blocking collectives: 163 us -> 0 us
  between operations: 15.7 us -> 0.75 us
  local copies, waits for them, and re-layouts: 17.3 us -> 26.2 us
  other arithmetic: 9.98 us -> 1.51 us
    reduce_scatter x5 -> x0, waiting for transfers between devices: 226 us -> none  [the longest x1 70.3 us: on_device(): lax.psum_scatter(grad_down[0], 'data', scatter_dimension=1, tiled=True)]
    pallas_call x0 -> x1, Pallas kernels: none -> 183 us  [on_device(): pl.pallas_call(functools.partial(kernel, n, bits, rows, orders), out_shap...]
    all_gather x4 -> x0, blocking collectives: 126 us -> none  [the longest x1 31.8 us: on_device(): lax.all_gather(new_key.astype(jnp.bfloat16), 'data', axis=0, tiled=True)]
    all_gather x2 -> x0, waiting for transfers between devices: 50.9 us -> none  [the longest x1 42.1 us: on_device(): lax.all_gather(new_down.astype(jnp.bfloat16), 'data', axis=1, tiled=True)]
    unnamed x2 -> x0, blocking collectives: 37.1 us -> none
    unnamed x9 -> x0, waiting for transfers between devices: 32.5 us -> none
    convert_element_type x7 -> x1, other arithmetic: 9.97 us -> 0.75 us  [on_device(): outs[6] = outs[6].reshape(-1).astype(jnp.bfloat16)]
    unnamed x59 -> x67, local copies, waits for them, and re-layouts: 17.2 us -> 24.9 us
  transfers between devices with their start and end apart: 8 -> 0, of which waited for: 8 -> 0; matrix products, arithmetic and copies ran while one was open for 4% -> 0% of each run, Pallas kernels for 0% -> 0%
where the time goes in v1:
time: 212 us; the launch traced here: 211 us
  Pallas kernels  183 us (86%)
  local copies, waits for them, and re-layouts  26.2 us (12%)
    pallas_call x1, Pallas kernels, on_device(): pl.pallas_call(functools.partial(kernel, n, bits, rows, orders), out_shap...  183 us
    unnamed x67, local copies, waits for them, and re-layouts  24.9 us

profile of v1, /device:TPU:0, one launch (start us, length us, event | category | flops | bytes accessed | tf_op | source)
XLA Modules:
  0.0 211.4 jit_solution(4596780637732861)
XLA Ops:
  0.7 0.8 reduce
  1.4 0.7 reshape.59.refs_6_
  2.1 1.9 copy.45.refs_8_
  4.0 1.9 copy.46.refs_15_
  5.9 1.1 copy.42
  7.1 1.1 copy.43
  8.3 1.1 copy.44
  9.4 183.0 %shard_map.364 = (bf16[768,768]{1,0:T(8,128)(2,1)}, bf16[768,768]{1,0:T(8,128)(2,1)}, bf16[768,192]{1,0:T(8,128)(2,1)}, bf16[768,192]{1,0:T(8,128)(2,1)}, bf16[7...) custom-call(f32[768,768]{1,0:T(8,128)} %bitcast.13, ...), custom_call_target="tpu_custom_call" | custom-call | tf_op jit(solution)/shard_map/pallas_call | solution.py:346
  192.4 0.7 convert_element_type.6
  193.1 0.7 convert_element_type.7
  193.8 1.9 copy.47
  195.7 1.9 copy.48
  197.6 0.9 copy.49
  198.5 0.9 copy.50
  199.3 0.9 copy.51
  200.2 1.0 copy.67
  201.2 0.7 copy-done
  201.9 1.0 copy.68
  202.9 0.1 copy-done.10
  203.1 0.7 copy.69
  203.8 0.7 copy.70
  204.5 0.6 copy.71
  205.2 0.6 copy.72
  205.8 0.6 copy.73
  206.5 0.6 copy.74
  207.1 0.5 copy.75
  207.6 0.7 copy.76
  208.3 0.6 copy.77
  209.0 0.6 copy.78
  209.6 0.6 copy.79
  210.3 0.6 copy.80
  210.9 0.5 copy.81
  (40 shorter events, 0.1 us)
Async XLA Ops:
  0.7 5.3 %copy-start.2 = (f32[1,768,192]{1,2,0:T(8,128)S(1)}, f32[1,768,192]{1,2,0:T(8,128)}, u32[]{:S(2)}) copy-start(f32[1,768,192]{1,2,0:T(8,128)} %param.23) | copy-start | bytes 1769476
  4.0 3.1 %copy-start.3 = (f32[1,768,192]{1,2,0:T(8,128)S(1)}, f32[1,768,192]{1,2,0:T(8,128)}, u32[]{:S(2)}) copy-start(f32[1,768,192]{1,2,0:T(8,128)} %param.24) | copy-start | bytes 1769476
  5.9 2.3 %copy-start.4 = (f32[1,768,192]{1,2,0:T(8,128)S(1)}, f32[1,768,192]{1,2,0:T(8,128)}, u32[]{:S(2)}) copy-start(f32[1,768,192]{1,2,0:T(8,128)} %param.25) | copy-start | bytes 1769476
  192.4 5.2 %copy-start.7 = (bf16[768,192]{1,0:T(8,128)(2,1)S(1)}, bf16[768,192]{1,0:T(8,128)(2,1)}, u32[]{:S(2)}) copy-start(bf16[768,192]{1,0:T(8,128)(2,1)} %get-tuple-element.67) | copy-start | bytes 884740
  192.4 6.1 %copy-start.6 = (f32[768,96]{1,0:T(8,128)S(1)}, f32[768,96]{1,0:T(8,128)}, u32[]{:S(2)}) copy-start(f32[768,96]{1,0:T(8,128)} %get-tuple-element.71) | copy-start | bytes 884740
  195.7 3.7 %copy-start.5 = (f32[768,96]{1,0:T(8,128)S(1)}, f32[768,96]{1,0:T(8,128)}, u32[]{:S(2)}) copy-start(f32[768,96]{1,0:T(8,128)} %get-tuple-element.78) | copy-start | bytes 884740
  197.6 2.6 %copy-start.1 = (bf16[768,768]{1,0:T(8,128)(2,1)S(1)}, bf16[768,768]{1,0:T(8,128)(2,1)}, u32[]{:S(2)}) copy-start(bf16[768,768]{1,0:T(8,128)(2,1)} %get-tuple-element.105) | copy-start | bytes 3538948
  200.2 1.7 copy-start
  201.9 1.1 copy-start.10
  201.9 1.9 copy-start.9
  203.0 1.5 copy-start.18
  203.1 2.1 %copy-start.17 = (f32[96,192]{1,0:T(8,128)S(1)}, f32[96,192]{1,0:T(8,128)}, u32[]{:S(2)}) copy-start(f32[96,192]{1,0:T(8,128)} %get-tuple-element.115) | copy-start | bytes 221188
  203.1 2.8 %copy-start.16 = (f32[96,192]{1,0:T(8,128)S(1)}, f32[96,192]{1,0:T(8,128)}, u32[]{:S(2)}) copy-start(f32[96,192]{1,0:T(8,128)} %get-tuple-element.116) | copy-start | bytes 221188
  203.1 3.4 %copy-start.15 = (f32[192,96]{1,0:T(8,128)S(1)}, f32[192,96]{1,0:T(8,128)}, u32[]{:S(2)}) copy-start(f32[192,96]{1,0:T(8,128)} %get-tuple-element.117) | copy-start | bytes 221188
  203.1 4.1 %copy-start.20 = (f32[1,96]{1,0:T(1,128)S(1)}, f32[1,96]{1,0:T(1,128)}, u32[]{:S(2)}) copy-start(f32[1,96]{1,0:T(1,128)} %get-tuple-element.55) | copy-start | bytes 1156
  203.1 4.6 %copy-start.8 = (f32[96,768]{1,0:T(8,128)S(1)}, f32[96,768]{1,0:T(8,128)}, u32[]{:S(2)}) copy-start(f32[96,768]{1,0:T(8,128)} %get-tuple-element.119) | copy-start | bytes 884740
  203.1 5.3 %copy-start.14 = (f32[96,192]{1,0:T(8,128)S(1)}, f32[96,192]{1,0:T(8,128)}, u32[]{:S(2)}) copy-start(f32[96,192]{1,0:T(8,128)} %get-tuple-element.121) | copy-start | bytes 221188
  203.8 5.2 %copy-start.13 = (f32[96,192]{1,0:T(8,128)S(1)}, f32[96,192]{1,0:T(8,128)}, u32[]{:S(2)}) copy-start(f32[96,192]{1,0:T(8,128)} %get-tuple-element.122) | copy-start | bytes 221188
  203.8 5.8 %copy-start.12 = (f32[96,192]{1,0:T(8,128)S(1)}, f32[96,192]{1,0:T(8,128)}, u32[]{:S(2)}) copy-start(f32[96,192]{1,0:T(8,128)} %get-tuple-element.123) | copy-start | bytes 221188
  203.8 6.5 %copy-start.11 = (f32[192,96]{1,0:T(8,128)S(1)}, f32[192,96]{1,0:T(8,128)}, u32[]{:S(2)}) copy-start(f32[192,96]{1,0:T(8,128)} %get-tuple-element.124) | copy-start | bytes 221188
  204.5 6.4 %copy-start.19 = (f32[1,96]{1,0:T(1,128)S(1)}, f32[1,96]{1,0:T(1,128)}, u32[]{:S(2)}) copy-start(f32[1,96]{1,0:T(1,128)} %get-tuple-element.62) | copy-start | bytes 1156

commit v2 on v1

--- a/solution.py
+++ b/solution.py
@@ -55,7 +55,7 @@
 
     mean_rate = n ** (-0.5)
     half = g_up.shape[1] // 2
-    heads = g_query.shape[1]
+    heads = g_query.shape[0]
     mine = tuple(bit[k] for k in reversed(range(bits)))
     every = (slice(None),) * bits
 
@@ -121,22 +121,10 @@
 
         return fill
 
-    def fill_pair(first, second, turned):
+    def fill_pair(first, second):
         def fill(chunk):
-            for d in range(n):
-                where = tuple((d >> k) & 1 for k in reversed(range(bits)))
-                if turned is None:
-
-                    def body(r):
-                        at = pl.ds(pl.multiple_of(d * rows + r, SUB), SUB)
-                        part[chunk][where + (pl.ds(r, SUB), slice(None))] = jnp.concatenate(
-                            [first[at, :], second[at, :]], axis=1
-                        )
-
-                    tile_loop(body)
-                else:
-                    at = slice(d * rows, (d + 1) * rows)
-                    part[chunk][where] = jnp.concatenate([first[at, :], turned[at, :]], axis=1)
+            both = turn(jnp.concatenate([first[...], second[...]], axis=0))
+            part[chunk][...] = blocks(both)
 
         return fill
 
@@ -154,25 +142,13 @@
     def own(chunk, lanes):
         return part[chunk][mine + (slice(None), lanes)]
 
-    def step_up(h):
+    def step_wide(h, weight, moment, n_out, s_out):
         def run(chunk):
             at = slice(h * half, (h + 1) * half)
-            new, state = update(own(chunk, slice(None)), w_up[:, at], m_up[:, at])
-            n_up[:, at] = new
-            s_up[:, at] = state
+            new, state = update(own(chunk, slice(None)), weight[:, at], moment[:, at])
+            n_out[:, at] = new
+            s_out[:, at] = state
             copies[chunk][mine] = new.astype(jnp.bfloat16)
-
-        return run
-
-    def step_down(h):
-        def run(chunk):
-            for j in range(half // LANES):
-                lanes = slice(j * LANES, (j + 1) * LANES)
-                at = slice(h * half + j * LANES, h * half + (j + 1) * LANES)
-                new, state = update(own(chunk, lanes), turn(w_down[at, :]), turn(m_down[at, :]))
-                copies[chunk][mine + (slice(None), lanes)] = new.astype(jnp.bfloat16)
-                n_down[at, :] = turn(new)
-                s_down[at, :] = turn(state)
 
         return run
 
@@ -233,21 +209,14 @@
 
         return end
 
-    def end_query_key(chunk):
-        def write(at, value):
-            value = value.astype(jnp.float32)
-            c_query[at, :] = value[:, :heads].astype(jnp.bfloat16)
-            c_key[at, :] = value[:, heads:].astype(jnp.bfloat16)
-
-        end_rows(chunk, write)
-
-    def end_value_mixed(chunk):
-        def write(at, value):
-            c_value[at, :] = value.astype(jnp.float32)[:, :heads].astype(jnp.bfloat16)
-
-        end_rows(chunk, write)
-        value = copies[chunk][...].astype(jnp.float32).reshape(n * rows, 2 * heads)
-        c_mixed[...] = turn(value[:, heads:]).astype(jnp.bfloat16)
+    def end_pair(first, second):
+        def end(chunk):
+            value = copies[chunk][...].astype(jnp.float32).reshape(n * rows, 2 * heads)
+            both = turn(value)
+            first[...] = both[:heads].astype(jnp.bfloat16)
+            second[...] = both[heads:].astype(jnp.bfloat16)
+
+        return end
 
     def end_norm(chunk):
         got = [
@@ -257,17 +226,14 @@
         for d in range(n):
             c_norm[d : d + 1, :] = got[d]
 
-    def fill_value_mixed(chunk):
-        fill_pair(g_value, None, turn(g_mixed[...]))(chunk)
-
     plan = [
-        (fill_up(0), step_up(0), end_up(0)),
-        (fill_up(1), step_up(1), end_up(1)),
+        (fill_up(0), step_wide(0, w_up, m_up, n_up, s_up), end_up(0)),
+        (fill_up(1), step_wide(1, w_up, m_up, n_up, s_up), end_up(1)),
         (fill_norm, step_norm, end_norm),
-        (fill_down(0), step_down(0), end_down(0)),
-        (fill_down(1), step_down(1), end_down(1)),
-        (fill_value_mixed, step_value_mixed, end_value_mixed),
-        (fill_pair(g_query, g_key, None), step_query_key, end_query_key),
+        (fill_down(0), step_wide(0, w_down, m_down, n_down, s_down), end_down(0)),
+        (fill_down(1), step_wide(1, w_down, m_down, n_down, s_down), end_down(1)),
+        (fill_pair(g_value, g_mixed), step_value_mixed, end_pair(c_value, c_mixed)),
+        (fill_pair(g_query, g_key), step_query_key, end_pair(c_query, c_key)),
     ]
 
     for chunk in range(count):
@@ -306,12 +272,25 @@
     ahead = []
     for chunk in range(count):
         for stage in range(2 * bits):
-            late = 0.5 * stage if stage < 2 * bits - 1 else max(0.5 * stage, count + 0.5 - 0.5 * chunk)
+            late = 0.75 * stage if stage < 2 * bits - 1 else max(0.5 * stage, count + 0.5 - 0.5 * chunk)
             ahead.append((chunk + late, chunk, stage))
     for _, chunk, stage in sorted(ahead):
         event(chunk, stage)
 
 
+def hand_on(count, *refs):
+    given, out, held, sem = refs[:count], refs[count : 2 * count], refs[2 * count : 3 * count], refs[3 * count]
+    reads = [pltpu.make_async_copy(given[i], held[i], sem.at[0, i]) for i in range(count)]
+    writes = [pltpu.make_async_copy(held[i], out[i], sem.at[1, i]) for i in range(count)]
+    for read in reads:
+        read.start()
+    for read, write in zip(reads, writes):
+        read.wait()
+        write.start()
+    for write in writes:
+        write.wait()
+
+
 def solution(mesh):
     n = mesh.shape["data"]
     bits = n.bit_length() - 1
@@ -319,15 +298,15 @@
     def on_device(*args):
         grads, weights, moments = args[:7], args[7:14], args[14:]
         rows = weights[0].shape[0]
-        grads = [g[0] for g in grads[:6]] + [grads[6].reshape(n, rows)]
+        grads = [g[0].T if i in (2, 3, 4) else g[0] for i, g in enumerate(grads[:6])] + [grads[6].reshape(n, rows)]
         weights = list(weights[:6]) + [weights[6].reshape(1, rows)]
         moments = list(moments[:6]) + [moments[6].reshape(1, rows)]
-        half, heads = grads[0].shape[1] // 2, grads[2].shape[1]
+        weights[1], moments[1] = weights[1].T, moments[1].T
+        half, heads = grads[0].shape[1] // 2, grads[2].shape[0]
         near = tuple(range(bits))
-        far = near[1:] + near[:1]
         wide = round_up(rows, LANES)
         sizes = [(rows, half)] * 2 + [(SUB, wide)] + [(rows, half)] * 2 + [(rows, 2 * heads)] * 2
-        orders = [far] + [near] * 6
+        orders = [near] * 7
         copy_sizes = [s if i != 2 else (16, wide) for i, s in enumerate(sizes)]
         shape = lambda a, dtype: jax.ShapeDtypeStruct(a.shape, dtype)
         out_shape = (
@@ -353,7 +332,18 @@
                 collective_id=0, has_side_effects=True, vmem_limit_bytes=60 * 2**20
             ),
         )(*grads, *weights, *moments)
+        count = len(outs)
+        anywhere = pl.BlockSpec(memory_space=pl.ANY)
+        outs = pl.pallas_call(
+            functools.partial(hand_on, count),
+            out_shape=out_shape,
+            in_specs=[anywhere] * count,
+            out_specs=[anywhere] * count,
+            scratch_shapes=[pltpu.VMEM(o.shape, o.dtype) for o in out_shape] + [pltpu.SemaphoreType.DMA((2, count))],
+        )(*outs)
         outs = list(outs)
+        for i in (2, 3, 4, 8, 15):
+            outs[i] = outs[i].T
         outs[6] = outs[6].reshape(-1).astype(jnp.bfloat16)
         outs[13] = outs[13].reshape(-1)
         outs[20] = outs[20].reshape(-1)

time: 212 us -> 139 us (0.66)
  Pallas kernels: 183 us -> 136 us
  local copies, waits for them, and re-layouts: 26.2 us -> 1.33 us
    pallas_call x1, Pallas kernels: 183 us -> 131 us  [on_device(): pl.pallas_call(functools.partial(kernel, n, bits, rows, orders), out_shap...]
    unnamed x67 -> x0, local copies, waits for them, and re-layouts: 24.9 us -> none
    pallas_call x0 -> x1, Pallas kernels: none -> 4.5 us  [on_device(): pl.pallas_call(functools.partial(hand_on, count), out_shape=out_shape, in...]
where the time goes in v2:
time: 139 us
  Pallas kernels  136 us (98%)
    pallas_call x1, Pallas kernels, on_device(): pl.pallas_call(functools.partial(kernel, n, bits, rows, orders), out_shap...  131 us
    pallas_call x1, Pallas kernels, on_device(): pl.pallas_call(functools.partial(hand_on, count), out_shape=out_shape, in...  4.5 us

profile of v2, /device:TPU:0, one launch (start us, length us, event | category | flops | bytes accessed | tf_op | source)
XLA Modules:
  0.0 138.9 jit_solution(8651692964650177521)
XLA Ops:
  0.7 0.7 reduce
  1.4 0.7 reshape.59.refs_6_
  2.0 131.0 %shard_map.364 = (bf16[768,768]{1,0:T(8,128)(2,1)}, bf16[768,768]{1,0:T(8,128)(2,1)}, bf16[192,768]{1,0:T(8,128)(2,1)}, bf16[192,768]{1,0:T(8,128)(2,1)}, bf16[1...) custom-call(f32[768,768]{1,0:T(8,128)} %bitcast.23, ...), custom_call_target="tpu_custom_call" | custom-call | tf_op jit(solution)/shard_map/pallas_call | solution.py:325
  133.0 4.5 %shard_map.365 = (bf16[768,768]{1,0:T(8,128)(2,1)}, bf16[768,768]{1,0:T(8,128)(2,1)}, bf16[192,768]{1,0:T(8,128)(2,1)}, bf16[192,768]{1,0:T(8,128)(2,1)}, bf16[1...) custom-call(bf16[768,768]{1,0:T(8,128)(2,1)} %get-tuple-element.63.r, ...), custom_call_target="tpu_custom_call" | custom-call | tf_op jit(solution)/shard_map/pallas_call | solution.py:337
  137.5 0.7 convert_element_type.6
  138.2 0.7 convert_element_type.7
